TPU v7x, 16 devices: a whole 2x2x2 slice. The times are simulated.
16 devices in a mesh: pod: 2 (over z), data: 8 (over y, x, core).
Axes of the slice: x: 2, y: 2, z: 2, core: 2. Of those that a mesh axis runs over, the one named last changes fastest.
Arguments:
- w_first: float32 [12, 768, 3072], replicated
- w_second: float32 [12, 3072, 768], replicated
- m_first: float32 [12, 768, 3072], replicated
- m_second: float32 [12, 3072, 768], replicated
- x_now: bfloat16 [8192, 768], P(('pod', 'data'))
- y_now: bfloat16 [8192, 768], P(('pod', 'data'))
- x_next: bfloat16 [8192, 768], P(('pod', 'data'))
- y_next: bfloat16 [8192, 768], P(('pod', 'data'))
Outputs:
- output 1: float32 [12, 768, 3072], replicated
- output 2: float32 [12, 3072, 768], replicated
- output 3: float32 [12, 768, 3072], replicated
- output 4: float32 [12, 3072, 768], replicated
- output 5: float32 [8192], P(('pod', 'data'))
- output 6: float32 [8192, 768], P(('pod', 'data'))
All inputs are finite; a program needn't handle non-finite values.
Results may differ from a plain program's by a relative error of at most 0.0108314.
Values are sent between devices in bfloat16 or wider.
A program may use at most 3.5 GiB of HBM per device.

v0:
```python
import jax
import jax.numpy as jnp
from jax import lax
from jax.sharding import PartitionSpec as P

LEARN_BASE = 0.25
MOMENTUM = 0.9


def solution(mesh):
    n_pod = mesh.shape['pod']
    n_data = mesh.shape['data']
    rows_spec = P(('pod', 'data'), None)
    full_spec = P()

    def reduce_grad(grad_low, scatter_dim):
        shard_sum = lax.psum_scatter(grad_low, 'data', scatter_dimension=scatter_dim, tiled=True)
        shard_sum = lax.psum(shard_sum, 'pod')
        return lax.all_gather(shard_sum, 'data', axis=scatter_dim, tiled=True).astype(jnp.float32)

    def train_step(w_first, w_second, m_first, m_second, x_now, y_now, x_next, y_next):
        layers = w_first.shape[0]
        model_width = w_first.shape[1]
        batch_total = x_now.shape[0] * n_pod * n_data
        learn_rate = LEARN_BASE / layers
        wf_low = w_first.astype(jnp.bfloat16)
        ws_low = w_second.astype(jnp.bfloat16)
        hidden = x_now.astype(jnp.float32)
        saved_acts = []
        for layer_idx in range(layers):
            h_low = hidden.astype(jnp.bfloat16)
            pre_act = jnp.dot(h_low, wf_low[layer_idx], preferred_element_type=jnp.float32)
            act_val, gelu_back = jax.vjp(jax.nn.gelu, pre_act)
            act_low = act_val.astype(jnp.bfloat16)
            hidden = hidden + jnp.dot(act_low, ws_low[layer_idx], preferred_element_type=jnp.float32)
            saved_acts.append((h_low, act_low, gelu_back))
        grad_h = (hidden - y_now.astype(jnp.float32)) / (batch_total * model_width)
        sum_first = [None] * layers
        sum_second = [None] * layers
        for layer_idx in reversed(range(layers)):
            h_low, act_low, gelu_back = saved_acts[layer_idx]
            grad_low = grad_h.astype(jnp.bfloat16)
            g_second = jnp.einsum('bf,bd->fd', act_low, grad_low, preferred_element_type=jnp.float32)
            grad_act = jnp.einsum('bd,fd->bf', grad_low, ws_low[layer_idx], preferred_element_type=jnp.float32)
            grad_pre = gelu_back(grad_act)[0].astype(jnp.bfloat16)
            g_first = jnp.einsum('bd,bf->df', h_low, grad_pre, preferred_element_type=jnp.float32)
            if layer_idx > 0:
                grad_h = grad_h + jnp.einsum('bf,df->bd', grad_pre, wf_low[layer_idx], preferred_element_type=jnp.float32)
            sum_second[layer_idx] = reduce_grad(g_second.astype(jnp.bfloat16), 0)
            sum_first[layer_idx] = reduce_grad(g_first.astype(jnp.bfloat16), 1)
        new_wf, new_ws, new_mf, new_ms = [], [], [], []
        hidden = x_next.astype(jnp.float32)
        for layer_idx in range(layers):
            mom_first = MOMENTUM * m_first[layer_idx] + sum_first[layer_idx]
            mom_second = MOMENTUM * m_second[layer_idx] + sum_second[layer_idx]
            weight_first = w_first[layer_idx] - learn_rate * mom_first
            weight_second = w_second[layer_idx] - learn_rate * mom_second
            new_mf.append(mom_first)
            new_ms.append(mom_second)
            new_wf.append(weight_first)
            new_ws.append(weight_second)
            pre_act = jnp.dot(hidden.astype(jnp.bfloat16), weight_first.astype(jnp.bfloat16), preferred_element_type=jnp.float32)
            act_low = jax.nn.gelu(pre_act).astype(jnp.bfloat16)
            hidden = hidden + jnp.dot(act_low, weight_second.astype(jnp.bfloat16), preferred_element_type=jnp.float32)
        resid_rows = hidden - y_next.astype(jnp.float32)
        loss_rows = jnp.sum(resid_rows * resid_rows, axis=-1) / (2 * model_width)
        return (jnp.stack(new_wf), jnp.stack(new_ws), jnp.stack(new_mf), jnp.stack(new_ms), loss_rows, hidden)

    return jax.shard_map(train_step, mesh=mesh,
                         in_specs=(full_spec,) * 4 + (rows_spec,) * 4,
                         out_specs=(full_spec,) * 4 + (P(('pod', 'data')), rows_spec),
                         check_vma=False)
```

profile of v0, /device:TPU:0, one launch (start us, length us, event | category | flops | bytes accessed | tf_op | source)
XLA Modules:
  0.0 3294.0 jit_solution(6753330227102474285)
XLA Ops:
  7.2 55.2 %convert_element_type.452 = bf16[12,3072,768]{2,1,0:T(8,128)(2,1)} convert(f32[12,3072,768]{2,1,0:T(8,128)} %param.9) | non-fusion elementwise | flops 28311552 | bytes 169869312 | tf_op jit(solution)/shard_map/convert_element_type | solution.py:27
  62.4 55.1 %convert_element_type.450 = bf16[12,768,3072]{2,1,0:T(8,128)(2,1)} convert(f32[12,768,3072]{2,1,0:T(8,128)} %param.8) | non-fusion elementwise | flops 28311552 | bytes 169869312 | tf_op jit(solution)/shard_map/convert_element_type | solution.py:26
  623.8 26.6 reduce-scatter.41.cloned.1.call-done
  650.4 51.1 %reduce-scatter.65.cloned.1.call-done = bf16[384,768]{1,0:T(8,128)(2,1)} async-done(((bf16[3072,768]{1,0:T(8,128)(2,1)}), bf16[384,768]{1,0:T(8,128)(2,1)}) %reduce-scatter.65.cloned.1.call-update) | async-done | bytes 589840 | tf_op jit(solution)/shard_map/reduce_scatter | solution.py:17
  701.6 51.2 %reduce-scatter.39.cloned.1.call-done = bf16[768,384]{0,1:T(8,128)(2,1)} async-done(((bf16[768,3072]{0,1:T(8,128)(2,1)}), bf16[768,384]{0,1:T(8,128)(2,1)}) %reduce-scatter.39.cloned.1.call-update) | async-done | bytes 589840 | tf_op jit(solution)/shard_map/reduce_scatter | solution.py:17
  752.7 51.0 %reduce-scatter.63.cloned.1.call-done = bf16[384,768]{1,0:T(8,128)(2,1)} async-done(((bf16[3072,768]{1,0:T(8,128)(2,1)}), bf16[384,768]{1,0:T(8,128)(2,1)}) %reduce-scatter.63.cloned.1.call-update) | async-done | bytes 589840 | tf_op jit(solution)/shard_map/reduce_scatter | solution.py:17
  803.7 51.2 %reduce-scatter.37.cloned.1.call-done = bf16[768,384]{0,1:T(8,128)(2,1)} async-done(((bf16[768,3072]{0,1:T(8,128)(2,1)}), bf16[768,384]{0,1:T(8,128)(2,1)}) %reduce-scatter.37.cloned.1.call-update) | async-done | bytes 589840 | tf_op jit(solution)/shard_map/reduce_scatter | solution.py:17
  854.9 51.0 %reduce-scatter.61.cloned.1.call-done = bf16[384,768]{1,0:T(8,128)(2,1)} async-done(((bf16[3072,768]{1,0:T(8,128)(2,1)}), bf16[384,768]{1,0:T(8,128)(2,1)}) %reduce-scatter.61.cloned.1.call-update) | async-done | bytes 589840 | tf_op jit(solution)/shard_map/reduce_scatter | solution.py:17
  905.9 51.2 %reduce-scatter.35.cloned.1.call-done = bf16[768,384]{0,1:T(8,128)(2,1)} async-done(((bf16[768,3072]{0,1:T(8,128)(2,1)}), bf16[768,384]{0,1:T(8,128)(2,1)}) %reduce-scatter.35.cloned.1.call-update) | async-done | bytes 589840 | tf_op jit(solution)/shard_map/reduce_scatter | solution.py:17
  957.1 51.0 %reduce-scatter.59.cloned.1.call-done = bf16[384,768]{1,0:T(8,128)(2,1)} async-done(((bf16[3072,768]{1,0:T(8,128)(2,1)}), bf16[384,768]{1,0:T(8,128)(2,1)}) %reduce-scatter.59.cloned.1.call-update) | async-done | bytes 589840 | tf_op jit(solution)/shard_map/reduce_scatter | solution.py:17
  1008.1 51.0 %reduce-scatter.33.cloned.1.call-done = bf16[768,384]{0,1:T(8,128)(2,1)} async-done(((bf16[768,3072]{0,1:T(8,128)(2,1)}), bf16[768,384]{0,1:T(8,128)(2,1)}) %reduce-scatter.33.cloned.1.call-update) | async-done | bytes 589840 | tf_op jit(solution)/shard_map/reduce_scatter | solution.py:17
  1059.1 51.0 %reduce-scatter.57.cloned.1.call-done = bf16[384,768]{1,0:T(8,128)(2,1)} async-done(((bf16[3072,768]{1,0:T(8,128)(2,1)}), bf16[384,768]{1,0:T(8,128)(2,1)}) %reduce-scatter.57.cloned.1.call-update) | async-done | bytes 589840 | tf_op jit(solution)/shard_map/reduce_scatter | solution.py:17
  1110.1 51.0 %reduce-scatter.31.cloned.1.call-done = bf16[768,384]{0,1:T(8,128)(2,1)} async-done(((bf16[768,3072]{0,1:T(8,128)(2,1)}), bf16[768,384]{0,1:T(8,128)(2,1)}) %reduce-scatter.31.cloned.1.call-update) | async-done | bytes 589840 | tf_op jit(solution)/shard_map/reduce_scatter | solution.py:17
  1161.1 51.0 %reduce-scatter.55.cloned.1.call-done = bf16[384,768]{1,0:T(8,128)(2,1)} async-done(((bf16[3072,768]{1,0:T(8,128)(2,1)}), bf16[384,768]{1,0:T(8,128)(2,1)}) %reduce-scatter.55.cloned.1.call-update) | async-done | bytes 589840 | tf_op jit(solution)/shard_map/reduce_scatter | solution.py:17
  1212.1 51.1 %reduce-scatter.29.cloned.1.call-done = bf16[768,384]{0,1:T(8,128)(2,1)} async-done(((bf16[768,3072]{0,1:T(8,128)(2,1)}), bf16[768,384]{0,1:T(8,128)(2,1)}) %reduce-scatter.29.cloned.1.call-update) | async-done | bytes 589840 | tf_op jit(solution)/shard_map/reduce_scatter | solution.py:17
  1263.3 51.0 %reduce-scatter.53.cloned.1.call-done = bf16[384,768]{1,0:T(8,128)(2,1)} async-done(((bf16[3072,768]{1,0:T(8,128)(2,1)}), bf16[384,768]{1,0:T(8,128)(2,1)}) %reduce-scatter.53.cloned.1.call-update) | async-done | bytes 589840 | tf_op jit(solution)/shard_map/reduce_scatter | solution.py:17
  1314.3 51.7 %reduce-scatter.27.cloned.1.call-done = bf16[768,384]{0,1:T(8,128)(2,1)} async-done(((bf16[768,3072]{0,1:T(8,128)(2,1)}), bf16[768,384]{0,1:T(8,128)(2,1)}) %reduce-scatter.27.cloned.1.call-update) | async-done | bytes 589840 | tf_op jit(solution)/shard_map/reduce_scatter | solution.py:17
  1366.0 51.2 %reduce-scatter.49.cloned.1.call-done = bf16[384,768]{1,0:T(8,128)(2,1)} async-done(((bf16[3072,768]{1,0:T(8,128)(2,1)}), bf16[384,768]{1,0:T(8,128)(2,1)}) %reduce-scatter.49.cloned.1.call-update) | async-done | bytes 589840 | tf_op jit(solution)/shard_map/reduce_scatter | solution.py:17
  1417.1 51.2 %reduce-scatter.51.cloned.1.call-done = bf16[384,768]{1,0:T(8,128)(2,1)} async-done(((bf16[3072,768]{1,0:T(8,128)(2,1)}), bf16[384,768]{1,0:T(8,128)(2,1)}) %reduce-scatter.51.cloned.1.call-update) | async-done | bytes 589840 | tf_op jit(solution)/shard_map/reduce_scatter | solution.py:17
  1468.3 51.6 %reduce-scatter.25.cloned.1.call-done = bf16[768,384]{0,1:T(8,128)(2,1)} async-done(((bf16[768,3072]{0,1:T(8,128)(2,1)}), bf16[768,384]{0,1:T(8,128)(2,1)}) %reduce-scatter.25.cloned.1.call-update) | async-done | bytes 589840 | tf_op jit(solution)/shard_map/reduce_scatter | solution.py:17
  1520.0 324.0 %all-reduce.3.cloned.1.call-done = (bf16[768,384]{0,1:T(8,128)(2,1)}, bf16[768,384]{0,1:T(8,128)(2,1)}, bf16[768,384]{0,1:T(8,128)(2,1)}, bf16[768,384]{0,1:T(8,...) async-done(((bf16[768,384]{0,1:T(8,128)(2,1)}, ...) | async-done | bytes 14155792 | tf_op jit(solution)/shard_map/psum | solution.py:18
  1859.0 72.4 %fusion.557 = (f32[1,768,3072]{2,1,0:T(8,128)}, f32[1,768,3072]{2,1,0:T(8,128)}, f32[1,768,3072]{2,1,0:T(8,128)}, f32[1,768,3072]{2,1,0:T(8,128)}, f32[1,768,307...) fusion(f32[12,768,3072]{2,1,0:T(8,128)} %param.10), kind=kLoop, calls=%fused_computation.638 | loop fusion | bytes 226492416 | tf_op jit(solution)/shard_map/slice | solution.py:54
  2046.6 72.4 %fusion.556 = (f32[1,768,3072]{2,1,0:T(8,128)}, f32[1,768,3072]{2,1,0:T(8,128)}, f32[1,768,3072]{2,1,0:T(8,128)}, f32[1,768,3072]{2,1,0:T(8,128)}, f32[1,768,307...) fusion(f32[12,768,3072]{2,1,0:T(8,128)} %param.8), kind=kLoop, calls=%fused_computation.637 | loop fusion | bytes 226492416 | tf_op jit(solution)/shard_map/slice | solution.py:56
  2234.4 18.2 convert_add_fusion
  2252.7 18.5 fusion.320
  2271.2 18.1 fusion.323
  2289.3 18.4 fusion.326
  2307.7 18.1 fusion.329
  2325.9 18.1 fusion.332
  2355.6 18.6 fusion.335
  2374.3 18.0 all-gather.39.cloned.1.call-done
  2392.3 36.6 %all-gather.63.cloned.1.call-done = bf16[3072,768]{1,0:T(8,128)(2,1)} async-done(((bf16[384,768]{1,0:T(8,128)(2,1)}), bf16[3072,768]{1,0:T(8,128)(2,1)}) %all-gather.63.cloned.1.call-update) | async-done | bytes 4718608 | tf_op jit(solution)/shard_map/all_gather | solution.py:19
  2428.9 18.0 fusion.338
  2446.9 18.6 all-gather.41.cloned.1.call-done
  2465.5 36.5 %all-gather.65.cloned.1.call-done = bf16[3072,768]{1,0:T(8,128)(2,1)} async-done(((bf16[384,768]{1,0:T(8,128)(2,1)}), bf16[3072,768]{1,0:T(8,128)(2,1)}) %all-gather.65.cloned.1.call-update) | async-done | bytes 4718608 | tf_op jit(solution)/shard_map/all_gather | solution.py:19
  2502.0 18.1 fusion.341
  2520.0 18.6 all-gather.43.cloned.1.call-done
  2538.6 36.5 %all-gather.67.cloned.1.call-done = bf16[3072,768]{1,0:T(8,128)(2,1)} async-done(((bf16[384,768]{1,0:T(8,128)(2,1)}), bf16[3072,768]{1,0:T(8,128)(2,1)}) %all-gather.67.cloned.1.call-update) | async-done | bytes 4718608 | tf_op jit(solution)/shard_map/all_gather | solution.py:19
  2575.1 19.3 fusion.344
  2594.4 17.2 all-gather.45.cloned.1.call-done
  2611.5 36.5 %all-gather.69.cloned.1.call-done = bf16[3072,768]{1,0:T(8,128)(2,1)} async-done(((bf16[384,768]{1,0:T(8,128)(2,1)}), bf16[3072,768]{1,0:T(8,128)(2,1)}) %all-gather.69.cloned.1.call-update) | async-done | bytes 4718608 | tf_op jit(solution)/shard_map/all_gather | solution.py:19
  2648.0 21.5 fusion.347
  2684.5 36.5 %all-gather.71.cloned.1.call-done = bf16[3072,768]{1,0:T(8,128)(2,1)} async-done(((bf16[384,768]{1,0:T(8,128)(2,1)}), bf16[3072,768]{1,0:T(8,128)(2,1)}) %all-gather.71.cloned.1.call-update) | async-done | bytes 4718608 | tf_op jit(solution)/shard_map/all_gather | solution.py:19
  2721.0 19.4 multiply_reduce_fusion
  2741.0 16.8 bitcast_dynamic-update-slice_fusion.23
  2901.6 109.3 %copy.51 = f32[12,768,3072]{2,1,0:T(8,128)} copy(f32[12,768,3072]{1,2,0:T(8,128)} %get-tuple-element.84) | data formatting | bytes 226492416
  3010.9 109.3 %copy.50 = f32[12,768,3072]{2,1,0:T(8,128)} copy(f32[12,768,3072]{1,2,0:T(8,128)} %get-tuple-element.85) | data formatting | bytes 226492416
  3120.2 16.1 bitcast_dynamic-update-slice_fusion.11
  (513 shorter events, 1071.1 us)
Async XLA Ops:
  7.2 616.5 %reduce-scatter.47.cloned.1.call-start = ((), (), s32[]{:S(2)}) async-start(), calls=%async_computation.46 | async-start | bytes 5308416 | tf_op jit(solution)/shard_map/reduce_scatter | solution.py:17
  293.3 330.4 %reduce-scatter.71.cloned.1.call-start = ((), (), s32[]{:S(2)}) async-start(), calls=%async_computation.70 | async-start | bytes 5308416 | tf_op jit(solution)/shard_map/reduce_scatter | solution.py:17
  302.1 321.6 %reduce-scatter.45.cloned.1.call-start = ((), (), s32[]{:S(2)}) async-start(), calls=%async_computation.44 | async-start | bytes 5308416 | tf_op jit(solution)/shard_map/reduce_scatter | solution.py:17
  324.3 299.4 %reduce-scatter.69.cloned.1.call-start = ((), (), s32[]{:S(2)}) async-start(), calls=%async_computation.68 | async-start | bytes 5308416 | tf_op jit(solution)/shard_map/reduce_scatter | solution.py:17
  333.4 290.3 %reduce-scatter.43.cloned.1.call-start = ((), (), s32[]{:S(2)}) async-start(), calls=%async_computation.42 | async-start | bytes 5308416 | tf_op jit(solution)/shard_map/reduce_scatter | solution.py:17
  364.8 285.6 %reduce-scatter.41.cloned.1.call-start = ((), (), s32[]{:S(2)}) async-start(), calls=%async_computation.40 | async-start | bytes 5308416 | tf_op jit(solution)/shard_map/reduce_scatter | solution.py:17
  386.5 315.1 %reduce-scatter.65.cloned.1.call-start = ((), (), s32[]{:S(2)}) async-start(), calls=%async_computation.64 | async-start | bytes 5308416 | tf_op jit(solution)/shard_map/reduce_scatter | solution.py:17
  395.9 356.8 %reduce-scatter.39.cloned.1.call-start = ((), (), s32[]{:S(2)}) async-start(), calls=%async_computation.38 | async-start | bytes 5308416 | tf_op jit(solution)/shard_map/reduce_scatter | solution.py:17
  415.6 388.1 %reduce-scatter.63.cloned.1.call-start = ((), (), s32[]{:S(2)}) async-start(), calls=%async_computation.62 | async-start | bytes 5308416 | tf_op jit(solution)/shard_map/reduce_scatter | solution.py:17
  424.6 430.3 %reduce-scatter.37.cloned.1.call-start = ((), (), s32[]{:S(2)}) async-start(), calls=%async_computation.36 | async-start | bytes 5308416 | tf_op jit(solution)/shard_map/reduce_scatter | solution.py:17
  444.4 461.5 %reduce-scatter.61.cloned.1.call-start = ((), (), s32[]{:S(2)}) async-start(), calls=%async_computation.60 | async-start | bytes 5308416 | tf_op jit(solution)/shard_map/reduce_scatter | solution.py:17
  453.4 503.7 %reduce-scatter.35.cloned.1.call-start = ((), (), s32[]{:S(2)}) async-start(), calls=%async_computation.34 | async-start | bytes 5308416 | tf_op jit(solution)/shard_map/reduce_scatter | solution.py:17
  473.1 535.0 %reduce-scatter.59.cloned.1.call-start = ((), (), s32[]{:S(2)}) async-start(), calls=%async_computation.58 | async-start | bytes 5308416 | tf_op jit(solution)/shard_map/reduce_scatter | solution.py:17
  482.3 576.8 %reduce-scatter.33.cloned.1.call-start = ((), (), s32[]{:S(2)}) async-start(), calls=%async_computation.32 | async-start | bytes 5308416 | tf_op jit(solution)/shard_map/reduce_scatter | solution.py:17
  502.0 608.1 %reduce-scatter.57.cloned.1.call-start = ((), (), s32[]{:S(2)}) async-start(), calls=%async_computation.56 | async-start | bytes 5308416 | tf_op jit(solution)/shard_map/reduce_scatter | solution.py:17
  511.0 650.1 %reduce-scatter.31.cloned.1.call-start = ((), (), s32[]{:S(2)}) async-start(), calls=%async_computation.30 | async-start | bytes 5308416 | tf_op jit(solution)/shard_map/reduce_scatter | solution.py:17
  530.7 681.4 %reduce-scatter.55.cloned.1.call-start = ((), (), s32[]{:S(2)}) async-start(), calls=%async_computation.54 | async-start | bytes 5308416 | tf_op jit(solution)/shard_map/reduce_scatter | solution.py:17
  539.7 723.6 %reduce-scatter.29.cloned.1.call-start = ((), (), s32[]{:S(2)}) async-start(), calls=%async_computation.28 | async-start | bytes 5308416 | tf_op jit(solution)/shard_map/reduce_scatter | solution.py:17
  559.4 754.9 %reduce-scatter.53.cloned.1.call-start = ((), (), s32[]{:S(2)}) async-start(), calls=%async_computation.52 | async-start | bytes 5308416 | tf_op jit(solution)/shard_map/reduce_scatter | solution.py:17
  568.6 797.4 %reduce-scatter.27.cloned.1.call-start = ((), (), s32[]{:S(2)}) async-start(), calls=%async_computation.26 | async-start | bytes 5308416 | tf_op jit(solution)/shard_map/reduce_scatter | solution.py:17
  588.3 828.9 %reduce-scatter.49.cloned.1.call-start = ((), (), s32[]{:S(2)}) async-start(), calls=%async_computation.48 | async-start | bytes 5308416 | tf_op jit(solution)/shard_map/reduce_scatter | solution.py:17
  603.3 865.0 %reduce-scatter.51.cloned.1.call-start = ((), (), s32[]{:S(2)}) async-start(), calls=%async_computation.50 | async-start | bytes 5308416 | tf_op jit(solution)/shard_map/reduce_scatter | solution.py:17
  611.8 908.1 %reduce-scatter.25.cloned.1.call-start = ((), (), s32[]{:S(2)}) async-start(), calls=%async_computation.24 | async-start | bytes 5308416 | tf_op jit(solution)/shard_map/reduce_scatter | solution.py:17
  623.6 1220.4 %all-reduce.3.cloned.1.call-start = ((), (), s32[]{:S(2)}) async-start(), calls=%async_computation.72 | async-start | bytes 28311552 | tf_op jit(solution)/shard_map/psum | solution.py:18
  1519.9 714.4 %all-gather.25.cloned.1.call-start = ((), (), s32[]{:S(2)}) async-start(), calls=%async_computation.25 | async-start | bytes 5308416 | tf_op jit(solution)/shard_map/all_gather | solution.py:19
  1844.0 390.4 %all-gather.49.cloned.1.call-start = ((), (), s32[]{:S(2)}) async-start(), calls=%async_computation.49 | async-start | bytes 5308416 | tf_op jit(solution)/shard_map/all_gather | solution.py:19
  1844.6 408.1 %all-gather.27.cloned.1.call-start = ((), (), s32[]{:S(2)}) async-start(), calls=%async_computation.27 | async-start | bytes 5308416 | tf_op jit(solution)/shard_map/all_gather | solution.py:19
  1845.3 407.4 %all-gather.51.cloned.1.call-start = ((), (), s32[]{:S(2)}) async-start(), calls=%async_computation.51 | async-start | bytes 5308416 | tf_op jit(solution)/shard_map/all_gather | solution.py:19
  1846.0 425.1 %all-gather.29.cloned.1.call-start = ((), (), s32[]{:S(2)}) async-start(), calls=%async_computation.29 | async-start | bytes 5308416 | tf_op jit(solution)/shard_map/all_gather | solution.py:19
  1846.6 424.6 %all-gather.53.cloned.1.call-start = ((), (), s32[]{:S(2)}) async-start(), calls=%async_computation.53 | async-start | bytes 5308416 | tf_op jit(solution)/shard_map/all_gather | solution.py:19
  1847.4 441.9 %all-gather.31.cloned.1.call-start = ((), (), s32[]{:S(2)}) async-start(), calls=%async_computation.31 | async-start | bytes 5308416 | tf_op jit(solution)/shard_map/all_gather | solution.py:19
  1848.1 441.2 %all-gather.55.cloned.1.call-start = ((), (), s32[]{:S(2)}) async-start(), calls=%async_computation.55 | async-start | bytes 5308416 | tf_op jit(solution)/shard_map/all_gather | solution.py:19
  1848.7 459.0 %all-gather.33.cloned.1.call-start = ((), (), s32[]{:S(2)}) async-start(), calls=%async_computation.33 | async-start | bytes 5308416 | tf_op jit(solution)/shard_map/all_gather | solution.py:19
  1849.4 458.3 %all-gather.57.cloned.1.call-start = ((), (), s32[]{:S(2)}) async-start(), calls=%async_computation.57 | async-start | bytes 5308416 | tf_op jit(solution)/shard_map/all_gather | solution.py:19
  1850.2 475.7 %all-gather.35.cloned.1.call-start = ((), (), s32[]{:S(2)}) async-start(), calls=%async_computation.35 | async-start | bytes 5308416 | tf_op jit(solution)/shard_map/all_gather | solution.py:19
  1850.8 475.1 %all-gather.59.cloned.1.call-start = ((), (), s32[]{:S(2)}) async-start(), calls=%async_computation.59 | async-start | bytes 5308416 | tf_op jit(solution)/shard_map/all_gather | solution.py:19
  1851.3 492.6 %all-gather.37.cloned.1.call-start = ((), (), s32[]{:S(2)}) async-start(), calls=%async_computation.37 | async-start | bytes 5308416 | tf_op jit(solution)/shard_map/all_gather | solution.py:19
  1852.1 503.5 %all-gather.61.cloned.1.call-start = ((), (), s32[]{:S(2)}) async-start(), calls=%async_computation.61 | async-start | bytes 5308416 | tf_op jit(solution)/shard_map/all_gather | solution.py:19
  1852.7 539.6 %all-gather.39.cloned.1.call-start = ((), (), s32[]{:S(2)}) async-start(), calls=%async_computation.39 | async-start | bytes 5308416 | tf_op jit(solution)/shard_map/all_gather | solution.py:19
  1853.4 575.5 %all-gather.63.cloned.1.call-start = ((), (), s32[]{:S(2)}) async-start(), calls=%async_computation.63 | async-start | bytes 5308416 | tf_op jit(solution)/shard_map/all_gather | solution.py:19
  1854.1 611.4 %all-gather.41.cloned.1.call-start = ((), (), s32[]{:S(2)}) async-start(), calls=%async_computation.41 | async-start | bytes 5308416 | tf_op jit(solution)/shard_map/all_gather | solution.py:19
  1854.9 647.1 %all-gather.65.cloned.1.call-start = ((), (), s32[]{:S(2)}) async-start(), calls=%async_computation.65 | async-start | bytes 5308416 | tf_op jit(solution)/shard_map/all_gather | solution.py:19
  1855.5 683.1 %all-gather.43.cloned.1.call-start = ((), (), s32[]{:S(2)}) async-start(), calls=%async_computation.43 | async-start | bytes 5308416 | tf_op jit(solution)/shard_map/all_gather | solution.py:19
  1856.2 718.9 %all-gather.67.cloned.1.call-start = ((), (), s32[]{:S(2)}) async-start(), calls=%async_computation.67 | async-start | bytes 5308416 | tf_op jit(solution)/shard_map/all_gather | solution.py:19
  1856.8 754.7 %all-gather.45.cloned.1.call-start = ((), (), s32[]{:S(2)}) async-start(), calls=%async_computation.45 | async-start | bytes 5308416 | tf_op jit(solution)/shard_map/all_gather | solution.py:19
  1857.4 790.6 %all-gather.69.cloned.1.call-start = ((), (), s32[]{:S(2)}) async-start(), calls=%async_computation.69 | async-start | bytes 5308416 | tf_op jit(solution)/shard_map/all_gather | solution.py:19
  1858.0 826.5 %all-gather.47.cloned.1.call-start = ((), (), s32[]{:S(2)}) async-start(), calls=%async_computation.47 | async-start | bytes 5308416 | tf_op jit(solution)/shard_map/all_gather | solution.py:19
  1858.5 862.4 %all-gather.71.cloned.1.call-start = ((), (), s32[]{:S(2)}) async-start(), calls=%async_computation.71 | async-start | bytes 5308416 | tf_op jit(solution)/shard_map/all_gather | solution.py:19
  (126 other events, 1891.2 us)
Sparse Core Ops, SparseCore 0:
  293.4 50.5 reduce-scatter.46
  347.3 47.7 reduce-scatter.70
  398.5 47.7 reduce-scatter.44
  449.5 47.7 reduce-scatter.68
  500.5 47.7 reduce-scatter.42
  551.5 47.7 reduce-scatter.66
  602.7 47.7 reduce-scatter.40
  653.8 47.7 reduce-scatter.64
  705.0 47.7 reduce-scatter.38
  756.0 47.7 reduce-scatter.62
  807.1 47.7 reduce-scatter.36
  858.2 47.7 reduce-scatter.60
  909.3 47.7 reduce-scatter.34
  960.4 47.7 reduce-scatter.58
  1011.4 47.7 reduce-scatter.32
  1062.4 47.7 reduce-scatter.56
  1113.4 47.7 reduce-scatter.30
  1164.4 47.6 reduce-scatter.54
  1215.5 47.7 reduce-scatter.28
  1266.5 47.7 reduce-scatter.52
  1318.2 47.7 reduce-scatter.26
  1369.4 47.7 reduce-scatter.48
  1420.6 47.7 reduce-scatter.50
  1472.1 47.7 reduce-scatter.24
  1525.4 318.4 all-reduce.2
  1845.6 34.7 all-gather.24
  1882.1 34.7 all-gather.48
  1918.7 34.7 all-gather.26
  1955.4 34.7 all-gather.50
  1991.8 34.7 all-gather.28
  2028.5 34.7 all-gather.52
  2065.1 34.7 all-gather.30
  2101.5 34.7 all-gather.54
  2138.2 34.7 all-gather.32
  2174.8 34.7 all-gather.56
  2211.3 34.7 all-gather.34
  2284.4 34.7 all-gather.36
  2320.8 34.7 all-gather.60
  2357.5 34.7 all-gather.38
  2394.1 34.7 all-gather.62
  2430.7 34.7 all-gather.40
  2467.2 34.7 all-gather.64
  2503.8 34.7 all-gather.42
  2540.3 34.7 all-gather.66
  2576.8 34.7 all-gather.44
  2613.2 34.7 all-gather.68
  2649.7 34.7 all-gather.46
  2686.2 34.7 all-gather.70
  (1 shorter events, 34.7 us)
where the time goes:
time: 3310 us; the launch traced here: 3290 us
  waiting for transfers between devices  1520 us (46%)
  matrix products  702 us (21%)
  local copies, waits for them, and re-layouts  631 us (19%)
  other arithmetic  423 us (13%)
    reduce_scatter x24, waiting for transfers between devices, reduce_grad(): lax.psum_scatter(grad_low, 'data', scatter_dimension=scatter_dim, tiled=T...  896 us
    unnamed x276, local copies, waits for them, and re-layouts  486 us
    psum x1, waiting for transfers between devices, reduce_grad(): shard_sum = lax.psum(shard_sum, 'pod')  324 us
    unnamed x49, other arithmetic  289 us
    all_gather x24, waiting for transfers between devices, reduce_grad(): lax.all_gather(shard_sum, 'data', axis=scatter_dim, tiled=True)  282 us
    dot_general x12, matrix products, train_step(): jnp.dot(act_low, weight_second.astype(jnp.bfloat16), preferred_element_ty...  224 us
    dot_general x12, matrix products, train_step(): jnp.einsum('bf,bd->fd', act_low, grad_low, preferred_element_type=jnp.flo...  105 us
    dot_general x12, matrix products, train_step(): jnp.dot(act_low, ws_low[layer_idx], preferred_element_type=jnp.float32)  98.4 us
  transfers between devices with their start and end apart: 49, of which 30 were waited for; matrix products, arithmetic and copies ran while one was open for 27% of the time, Pallas kernels for 0%

commit v1 on v0

v1 whole, which is shorter than its diff:
```python
import functools

import jax
import jax.numpy as jnp
from jax import lax
from jax.experimental import pallas as pl
from jax.experimental.pallas import tpu as pltpu
from jax.sharding import PartitionSpec as P

LEARN_BASE = 0.25
MOMENTUM = 0.9
GELU_C = 0.7978845608028654
GELU_A = 0.044715
BF = jnp.bfloat16
F32 = jnp.float32
MESH_ID = pl.DeviceIdType.MESH
BLK = 768
HALF = BLK // 2
PART = HALF // 3
NACC = 4
NFULL = 6
CHUNK = 256
NN = (((1,), (0,)), ((), ()))
NT = (((1,), (1,)), ((), ()))


def dot(lhs, rhs, dims=NN):
    return lax.dot_general(lhs, rhs, dims, preferred_element_type=F32)


def gelu(a):
    return a * (0.5 * (1.0 + jnp.tanh(GELU_C * (a + GELU_A * (a * a * a)))))


def gelu_pair(a):
    sq = a * a
    t = jnp.tanh(GELU_C * (a + GELU_A * (sq * a)))
    cdf = 0.5 * (1.0 + t)
    slope = cdf + a * (0.5 * (1.0 - t * t)) * (GELU_C * (1.0 + (3.0 * GELU_A) * sq))
    return a * cdf, slope


def step_kernel(layers, per_layer, scale, learn_rate,
                w1, w2, m1, m2, x_now, y_now, x_next,
                g1, g2, hs, h_out,
                wbuf, mbuf, gst, gfull, acc, land0, land1, land2, land3,
                hl, hl_t, low, state, actq, wlow, rows_in,
                ld_sem, hs_sem, io_sem, st_sem, own_sem,
                x0_s, x0_r, rs_s, rs_r, ag_s, ag_r, x7_s, x7_r, out_sem):
    units = layers * per_layer
    pod = lax.axis_index('pod')
    data = lax.axis_index('data')
    core = lax.rem(data, 2)
    cx = lax.rem(data // 2, 2)
    cy = data // 4
    partner = (pod, data + 1 - 2 * core)
    along = {'x': (cx, (pod, data + 2 - 4 * cx)),
             'y': (cy, (pod, data + 4 - 8 * cy)),
             'z': (pod, (1 - pod, data))}
    orders = ('xyz', 'yzx', 'zxy')

    barrier = pltpu.get_barrier_semaphore()
    for dev in (partner, along['x'][1], along['y'][1], along['z'][1]):
        pl.semaphore_signal(barrier, inc=1, device_id=dev, device_id_type=MESH_ID)
    pl.semaphore_wait(barrier, 4)

    def block_of(ref, k, layer, f):
        off = pl.multiple_of(f * BLK, BLK)
        if k == 0:
            return ref.at[layer, :, pl.ds(off, BLK)]
        return ref.at[layer, pl.ds(off, BLK), :]

    def loads(layer, f, par, full):
        out = []
        for k in range(2):
            out.append(pltpu.make_async_copy(block_of((w1, w2)[k], k, layer, f), wbuf.at[k, par], ld_sem.at[par, k]))
            if full:
                out.append(pltpu.make_async_copy(block_of((m1, m2)[k], k, layer, f), mbuf.at[k, par], ld_sem.at[par, 2 + k]))
                out.append(pltpu.make_async_copy(block_of((g1, g2)[k], k, layer, f), gst.at[k, par], ld_sem.at[par, 4 + k]))
        return out

    def start_all(copies):
        for c in copies:
            c.start()

    def wait_all(copies):
        for c in copies:
            c.wait()

    def cast_weights(par, full):
        def body(r, _):
            rows = pl.ds(pl.multiple_of(r * 64, 64), 64)
            for k in range(2):
                w = wbuf[k, par, rows, :]
                if full:
                    mom = MOMENTUM * mbuf[k, par, rows, :] + gst[k, par, rows, :].astype(F32)
                    w = w - learn_rate * mom
                wlow[k, rows, :] = w.astype(BF)
            return 0
        lax.fori_loop(0, BLK // 64, body, 0)

    def col(j):
        return pl.ds(pl.multiple_of(j * CHUNK, CHUNK), CHUNK)

    def load_rows(src):
        copy = pltpu.make_async_copy(src, rows_in, io_sem.at[0])
        copy.start()
        copy.wait()

    def save_h(layer):
        return pltpu.make_async_copy(low, hs.at[layer], hs_sem.at[0])

    def fetch_h(layer):
        slot = lax.rem(layer, 2)
        return pltpu.make_async_copy(hs.at[layer], hl.at[slot], hs_sem.at[slot])

    def forward_unit(i, full):
        layer, f, par = i // per_layer, lax.rem(i, per_layer), lax.rem(i, 2)
        wait_all(loads(layer, f, par, full))

        @pl.when(i + 1 < units)
        def _():
            nxt = i + 1
            start_all(loads(nxt // per_layer, lax.rem(nxt, per_layer), lax.rem(nxt, 2), full))

        @pl.when(f == 0)
        def _():
            if not full:
                @pl.when(layer > 0)
                def _():
                    save_h(layer - 1).wait()
            low[...] = state[...].astype(BF)
            if not full:
                save_h(layer).start()

        cast_weights(par, full)

        def first(j, _):
            a = dot(low[...], wlow[0, :, col(j)])
            actq[:, col(j)] = gelu(a).astype(BF)
            return 0
        lax.fori_loop(0, BLK // CHUNK, first, 0)

        def second(j, _):
            state[:, col(j)] += dot(actq[...], wlow[1, :, col(j)])
            return 0
        lax.fori_loop(0, BLK // CHUNK, second, 0)

    def back_place(b):
        return layers - 1 - b // per_layer, lax.rem(b, per_layer), lax.rem(b, 2)

    def store_grads(b):
        layer, f, par = back_place(b)
        return [pltpu.make_async_copy(gst.at[k, par], block_of((g1, g2)[k], k, layer, f), st_sem.at[par, k])
                for k in range(2)]

    def backward_unit(b):
        layer, f, par = back_place(b)
        wait_all(loads(layer, f, par, False))

        @pl.when(b + 1 < units)
        def _():
            nl, nf, np_ = back_place(b + 1)
            start_all(loads(nl, nf, np_, False))

        slot = lax.rem(layer, 2)

        @pl.when(f == 0)
        def _():
            fetch_h(layer).wait()

            @pl.when(layer > 0)
            def _():
                fetch_h(layer - 1).start()
            low[...] = state[...].astype(BF)
            hl_t[...] = hl[slot].T

        cast_weights(par, False)

        @pl.when(b >= 2)
        def _():
            wait_all(store_grads(b - 2))

        def body(j, _):
            a = dot(hl[slot], wlow[0, :, col(j)])
            du = dot(low[...], wlow[1, col(j), :], NT)
            u, slope = gelu_pair(a)
            q = (slope * du).astype(BF)
            actq[:, col(j)] = q
            gst[1, par, col(j), :] = dot(u.astype(BF).T, low[...]).astype(BF)
            gst[0, par, :, col(j)] = dot(hl_t[...], q).astype(BF)
            return 0
        lax.fori_loop(0, BLK // CHUNK, body, 0)

        @pl.when(layer > 0)
        def _():
            def carry(j, _):
                state[:, col(j)] += dot(actq[...], wlow[0, col(j), :], NT)
                return 0
            lax.fori_loop(0, BLK // CHUNK, carry, 0)
        start_all(store_grads(b))

    back_ticks = units // 3
    early = back_ticks // per_layer

    def comm_place(c):
        s = c // per_layer
        layer = jnp.where(s == 0, layers - 1,
                          jnp.where(s < early, layers - 2 - s,
                                    jnp.where(s < layers - 1, s - early, layers - 2)))
        return layer, lax.rem(c, per_layer)

    def x0_copies(c):
        layer, f = comm_place(c)
        out = []
        par = lax.rem(c, 2)
        slot = lax.rem(c, NACC)
        for k in range(2):
            def rows_of(start):
                if k == 0:
                    return g1.at[layer, pl.ds(pl.multiple_of(start, HALF), HALF), pl.ds(pl.multiple_of(f * BLK, BLK), BLK)]
                return g2.at[layer, pl.ds(pl.multiple_of(f * BLK + start, HALF), HALF), :]
            out.append(pltpu.make_async_remote_copy(
                src_ref=rows_of((1 - core) * HALF), dst_ref=land0.at[par, k],
                send_sem=x0_s.at[par, k], recv_sem=x0_r.at[par, k],
                device_id=partner, device_id_type=MESH_ID))
            out.append(pltpu.make_async_copy(rows_of(core * HALF), acc.at[slot, k], own_sem.at[par, k]))
        return out

    def offsets(p):
        coords = [along[a][0] for a in orders[p]]
        keep1 = p * PART + coords[0] * (PART // 2)
        send1 = p * PART + (1 - coords[0]) * (PART // 2)
        keep2 = keep1 + coords[1] * (PART // 4)
        send2 = keep1 + (1 - coords[1]) * (PART // 4)
        keep3 = keep2 + coords[2] * (PART // 8)
        send3 = keep2 + (1 - coords[2]) * (PART // 8)
        return (keep1, keep2, keep3), (send1, send2, send3)

    places = [offsets(p) for p in range(3)]
    lands = (land1, land2, land3)
    sizes = (PART // 2, PART // 4, PART // 8)

    def rs_copies(c, j):
        par, slot = lax.rem(c, 2), lax.rem(c, NACC)
        n = sizes[j]
        return [pltpu.make_async_remote_copy(
            src_ref=acc.at[slot, :, pl.ds(pl.multiple_of(places[p][1][j], 16), n), :],
            dst_ref=lands[j].at[par, :, pl.ds(p * n, n), :],
            send_sem=rs_s.at[j, par, p], recv_sem=rs_r.at[j, par, p],
            device_id=along[orders[p][j]][1], device_id_type=MESH_ID) for p in range(3)]

    def ag_copies(c, j):
        par, slot = lax.rem(c, 2), lax.rem(c, NFULL)
        n = sizes[2 - j]
        out = []
        for p in range(3):
            rows = pl.ds(pl.multiple_of(core * HALF + places[p][0][2 - j], 16), n)
            out.append(pltpu.make_async_remote_copy(
                src_ref=gfull.at[slot, :, rows, :], dst_ref=gfull.at[slot, :, rows, :],
                send_sem=ag_s.at[j, par, p], recv_sem=ag_r.at[j, par, p],
                device_id=along[orders[p][2 - j]][1], device_id_type=MESH_ID))
        return out

    def x7_copies(c):
        par, slot = lax.rem(c, 2), lax.rem(c, NFULL)
        rows = pl.ds(pl.multiple_of(core * HALF, HALF), HALF)
        return [pltpu.make_async_remote_copy(
            src_ref=gfull.at[slot, :, rows, :], dst_ref=gfull.at[slot, :, rows, :],
            send_sem=x7_s.at[par], recv_sem=x7_r.at[par],
            device_id=partner, device_id_type=MESH_ID)]

    def out_copies(c):
        layer, f = comm_place(c)
        par, slot = lax.rem(c, 2), lax.rem(c, NFULL)
        return [pltpu.make_async_copy(gfull.at[slot, k], block_of((g1, g2)[k], k, layer, f), out_sem.at[par, k])
                for k in range(2)]

    def stage(c, s):
        @pl.when((c >= 0) & (c < units))
        def _():
            par, slot = lax.rem(c, 2), lax.rem(c, NACC)
            if s == 0:
                start_all(x0_copies(c))
            elif s == 1:
                wait_all(x0_copies(c))

                def body(r, _):
                    rows = pl.ds(pl.multiple_of(r * 64, 64), 64)
                    for k in range(2):
                        acc[slot, k, rows, :] = (acc[slot, k, rows, :].astype(F32)
                                                 + land0[par, k, rows, :].astype(F32)).astype(BF)
                    return 0
                lax.fori_loop(0, HALF // 64, body, 0)
                start_all(rs_copies(c, 0))
            elif s in (2, 3, 4):
                j = s - 2
                copies = rs_copies(c, j)
                n = sizes[j]
                full_slot = lax.rem(c, NFULL)
                for p in range(3):
                    copies[p].wait()
                    rows = pl.ds(pl.multiple_of(places[p][0][j], 16), n)
                    for k in range(2):
                        total = (acc[slot, k, rows, :].astype(F32)
                                 + lands[j][par, k, p * n:(p + 1) * n, :].astype(F32)).astype(BF)
                        if s < 4:
                            acc[slot, k, rows, :] = total
                        else:
                            own = pl.ds(pl.multiple_of(core * HALF + places[p][0][j], 16), n)
                            gfull[full_slot, k, own, :] = total
                start_all(rs_copies(c, j + 1) if s < 4 else ag_copies(c, 0))
            elif s in (5, 6):
                wait_all(ag_copies(c, s - 5))
                start_all(ag_copies(c, s - 4))
            elif s == 7:
                wait_all(ag_copies(c, 2))
                start_all(x7_copies(c))
            elif s == 8:
                wait_all(x7_copies(c))
                start_all(out_copies(c))
            else:
                wait_all(out_copies(c))

    start_all(loads(0, 0, 0, False))
    load_rows(x_now)
    state[...] = rows_in[...].astype(F32)

    def fwd_now(i, _):
        forward_unit(i, False)
        return 0
    lax.fori_loop(0, units, fwd_now, 0)
    save_h(layers - 1).wait()
    fetch_h(layers - 1).start()
    start_all(loads(layers - 1, 0, 0, False))
    load_rows(y_now)
    state[...] = (state[...] - rows_in[...].astype(F32)) * scale

    late = (layers - 1 - early) * per_layer
    first_tick = back_ticks + 10
    burst_tick = first_tick + late
    burst = (early - 1) * per_layer // 3
    last_tick = burst_tick + burst

    def tick(t, _):
        for s in (9, 8, 7, 6, 5):
            stage(t - s, s)

        def back(j, _):
            backward_unit(3 * t + j)
            return 0
        lax.fori_loop(0, jnp.where(t < back_ticks, 3, 0), back, 0)

        @pl.when(t == back_ticks)
        def _():
            wait_all(store_grads(units - 2))
            wait_all(store_grads(units - 1))

        @pl.when(t == first_tick - 1)
        def _():
            start_all(loads(0, 0, 0, True))
            load_rows(x_next)
            state[...] = rows_in[...].astype(F32)

        count = jnp.where(t < first_tick, 0, jnp.where(t < burst_tick, 1, jnp.where(t < last_tick, 3, 2 * per_layer)))
        begin = jnp.where(t < burst_tick, t - first_tick,
                          jnp.where(t < last_tick, late + 3 * (t - burst_tick), late + 3 * burst))

        def ahead(j, _):
            forward_unit(begin + j, True)
            return 0
        lax.fori_loop(0, count, ahead, 0)

        for s in (4, 3, 2, 1, 0):
            stage(t - s, s)
        return 0
    lax.fori_loop(0, last_tick + 1, tick, 0)

    copy = pltpu.make_async_copy(state, h_out, io_sem.at[0])
    copy.start()
    copy.wait()


def build_kernel(w_first, rows, batch_total, learn_rate):
    layers, width, hidden = w_first.shape
    per_layer = hidden // BLK
    any_spec = pl.BlockSpec(memory_space=pl.ANY)
    dma = pltpu.SemaphoreType.DMA
    return pl.pallas_call(
        functools.partial(step_kernel, layers, per_layer, 1.0 / (batch_total * width), learn_rate),
        out_shape=(jax.ShapeDtypeStruct((layers, width, hidden), BF),
                   jax.ShapeDtypeStruct((layers, hidden, width), BF),
                   jax.ShapeDtypeStruct((layers, rows, width), BF),
                   jax.ShapeDtypeStruct((rows, width), F32)),
        in_specs=[any_spec] * 7,
        out_specs=(any_spec,) * 4,
        scratch_shapes=[
            pltpu.VMEM((2, 2, BLK, BLK), F32),
            pltpu.VMEM((2, 2, BLK, BLK), F32),
            pltpu.VMEM((2, 2, BLK, BLK), BF),
            pltpu.VMEM((NFULL, 2, BLK, BLK), BF),
            pltpu.VMEM((NACC, 2, HALF, BLK), BF),
            pltpu.VMEM((2, 2, HALF, BLK), BF),
            pltpu.VMEM((2, 2, HALF // 2, BLK), BF),
            pltpu.VMEM((2, 2, HALF // 4, BLK), BF),
            pltpu.VMEM((2, 2, HALF // 8, BLK), BF),
            pltpu.VMEM((2, rows, width), BF),
            pltpu.VMEM((width, rows), BF),
            pltpu.VMEM((rows, width), BF),
            pltpu.VMEM((rows, width), F32),
            pltpu.VMEM((rows, BLK), BF),
            pltpu.VMEM((2, BLK, BLK), BF),
            pltpu.VMEM((rows, width), BF),
            dma((2, 6)), dma((2,)), dma((1,)), dma((2, 2)), dma((2, 2)),
            dma((2, 2)), dma((2, 2)), dma((3, 2, 3)), dma((3, 2, 3)), dma((3, 2, 3)), dma((3, 2, 3)),
            dma((2,)), dma((2,)), dma((2, 2)),
        ],
        compiler_params=pltpu.CompilerParams(collective_id=0, has_side_effects=True, vmem_limit_bytes=66_000_000),
    )


def solution(mesh):
    n_dev = mesh.shape['pod'] * mesh.shape['data']
    rows_spec = P(('pod', 'data'), None)
    full_spec = P()

    def train_step(w_first, w_second, m_first, m_second, x_now, y_now, x_next, y_next):
        layers, model_width, _ = w_first.shape
        rows = x_now.shape[0]
        learn_rate = LEARN_BASE / layers
        kernel = build_kernel(w_first, rows, rows * n_dev, learn_rate)
        g_first, g_second, _, hidden = kernel(w_first, w_second, m_first, m_second, x_now, y_now, x_next)
        mom_first = MOMENTUM * m_first + g_first.astype(F32)
        mom_second = MOMENTUM * m_second + g_second.astype(F32)
        weight_first = w_first - learn_rate * mom_first
        weight_second = w_second - learn_rate * mom_second
        resid_rows = hidden - y_next.astype(F32)
        loss_rows = jnp.sum(resid_rows * resid_rows, axis=-1) / (2 * model_width)
        return weight_first, weight_second, mom_first, mom_second, loss_rows, hidden

    return jax.shard_map(train_step, mesh=mesh,
                         in_specs=(full_spec,) * 4 + (rows_spec,) * 4,
                         out_specs=(full_spec,) * 4 + (P(('pod', 'data')), rows_spec),
                         check_vma=False)
```

time: 3310 us -> 1400 us (0.42)
  waiting for transfers between devices: 1520 us -> 0 us
  Pallas kernels: 0 us -> 1060 us
  matrix products: 702 us -> 0 us
  local copies, waits for them, and re-layouts: 631 us -> 1.15 us
  other arithmetic: 423 us -> 331 us
    pallas_call x0 -> x1, Pallas kernels: none -> 1060 us  [train_step(): kernel(w_first, w_second, m_first, m_second, x_now, y_now, x_next)]
    reduce_scatter x24 -> x0, waiting for transfers between devices: 896 us -> none  [reduce_grad(): lax.psum_scatter(grad_low, 'data', scatter_dimension=scatter_dim, tiled=T...]
    dot_general x82 -> x0, matrix products: 702 us -> none  [the longest x12 224 us: train_step(): jnp.dot(act_low, weight_second.astype(jnp.bfloat16), preferred_element_ty...]
    unnamed x276 -> x5, local copies, waits for them, and re-layouts: 486 us -> 1.15 us
    sub x0 -> x2, other arithmetic: none -> 330 us  [the longest x1 167 us: train_step(): weight_first = w_first - learn_rate * mom_first]
    psum x1 -> x0, waiting for transfers between devices: 324 us -> none  [reduce_grad(): shard_sum = lax.psum(shard_sum, 'pod')]
    unnamed x49 -> x0, other arithmetic: 289 us -> none
    all_gather x24 -> x0, waiting for transfers between devices: 282 us -> none  [reduce_grad(): lax.all_gather(shard_sum, 'data', axis=scatter_dim, tiled=True)]
  transfers between devices with their start and end apart: 49 -> 0, of which waited for: 30 -> 0; matrix products, arithmetic and copies ran while one was open for 27% -> 0% of each run, Pallas kernels for 0% -> 0%
where the time goes in v1:
time: 1400 us
  Pallas kernels  1060 us (76%)
  other arithmetic  331 us (24%)
    pallas_call x1, Pallas kernels, train_step(): kernel(w_first, w_second, m_first, m_second, x_now, y_now, x_next)  1060 us
    sub x1, other arithmetic, train_step(): weight_first = w_first - learn_rate * mom_first  167 us
    sub x1, other arithmetic, train_step(): weight_second = w_second - learn_rate * mom_second  164 us

profile of v1, /device:TPU:0, one launch (start us, length us, event | category | flops | bytes accessed | tf_op | source)
XLA Modules:
  0.0 1397.8 jit_solution(10710988548785179306)
XLA Ops:
  0.6 1064.7 %shard_map.127 = (bf16[12,768,3072]{2,1,0:T(8,128)(2,1)}, bf16[12,3072,768]{2,1,0:T(8,128)(2,1)}, bf16[12,512,768]{2,1,0:T(8,128)(2,1)}, f32[512,768]{1,0:T(8,128)}) custom-call(f32[12,768,3072]{2,1,0:T(8,128)} %w1.1, f32[12,3072,768]{2,1,0:T(8,128)} %w2.1, f32[12,768,3072]{2,1,0:T(8,128)} %m1.1, f32[12,3072,768]{2,1,0:T(8,128)} %m2.1, ...), custom_call_target="tpu_custom_call" | custom-call | tf_op jit(solution)/shard_map/pallas_call | solution.py:432
  1065.3 166.6 %multiply_subtract_fusion.1 = (f32[12,768,3072]{2,1,0:T(8,128)}, f32[12,768,3072]{2,1,0:T(8,128)}) fusion(f32[12,768,3072]{2,1,0:T(8,128)} %w1.1, bf16[12,768,3072]{2,1,0:T(8,128)(2,1)} %get-tuple-element.9, f32[12,768,3072]{2,1,0:T(8,128)} %m1.1), kind=kLoop, calls=%fused_computation.2 | loop fusion | flops 141557760 | bytes 509607936 | tf_op jit(solution)/shard_map/sub | solution.py:435
  1231.9 0.0 copy-start
  1231.9 0.0 copy-start.1
  1231.9 163.9 %multiply_subtract_fusion = (f32[12,3072,768]{2,1,0:T(8,128)}, f32[12,3072,768]{2,1,0:T(8,128)}) fusion(f32[12,3072,768]{2,1,0:T(8,128)} %w2.1, bf16[12,3072,768]{2,1,0:T(8,128)(2,1)} %get-tuple-element.10, f32[12,3072,768]{2,1,0:T(8,128)} %m2.1), kind=kLoop, calls=%fused_computation | loop fusion | flops 141557760 | bytes 509607936 | tf_op jit(solution)/shard_map/sub | solution.py:436
  1395.8 0.0 copy-done
  1395.8 0.0 copy-done.1
  1395.8 0.3 multiply_reduce_fusion
  1396.1 0.6 broadcast_multiply_fusion
  1396.7 1.1 copy.15
Async XLA Ops:
  1231.9 163.9 %copy-start = (f32[512,768]{1,0:T(8,128)S(1)}, f32[512,768]{1,0:T(8,128)}, u32[]{:S(2)}) copy-start(f32[512,768]{1,0:T(8,128)} %get-tuple-element.27) | copy-start | bytes 4718596
  1231.9 163.9 %copy-start.1 = (bf16[512,768]{1,0:T(8,128)(2,1)S(1)}, bf16[512,768]{1,0:T(8,128)(2,1)}, u32[]{:S(2)}) copy-start(bf16[512,768]{1,0:T(8,128)(2,1)} %param.15) | copy-start | bytes 2359300

commit v2 on v1

--- a/solution.py
+++ b/solution.py
@@ -20,6 +20,8 @@
 NACC = 4
 NFULL = 6
 CHUNK = 256
+BACK_RATE = 2
+BURST_RATE = 4
 NN = (((1,), (0,)), ((), ()))
 NT = (((1,), (1,)), ((), ()))
 
@@ -200,7 +202,7 @@
             lax.fori_loop(0, BLK // CHUNK, carry, 0)
         start_all(store_grads(b))
 
-    back_ticks = units // 3
+    back_ticks = units // BACK_RATE
     early = back_ticks // per_layer
 
     def comm_place(c):
@@ -337,19 +339,19 @@
     state[...] = (state[...] - rows_in[...].astype(F32)) * scale
 
     late = (layers - 1 - early) * per_layer
-    first_tick = back_ticks + 10
+    first_tick = back_ticks + 11
     burst_tick = first_tick + late
-    burst = (early - 1) * per_layer // 3
+    burst = (early - 1) * per_layer // BURST_RATE
     last_tick = burst_tick + burst
 
     def tick(t, _):
         for s in (9, 8, 7, 6, 5):
-            stage(t - s, s)
+            stage(t - 1 - s, s)
 
         def back(j, _):
-            backward_unit(3 * t + j)
-            return 0
-        lax.fori_loop(0, jnp.where(t < back_ticks, 3, 0), back, 0)
+            backward_unit(BACK_RATE * t + j)
+            return 0
+        lax.fori_loop(0, jnp.where(t < back_ticks, BACK_RATE, 0), back, 0)
 
         @pl.when(t == back_ticks)
         def _():
@@ -362,9 +364,9 @@
             load_rows(x_next)
             state[...] = rows_in[...].astype(F32)
 
-        count = jnp.where(t < first_tick, 0, jnp.where(t < burst_tick, 1, jnp.where(t < last_tick, 3, 2 * per_layer)))
+        count = jnp.where(t < first_tick, 0, jnp.where(t < burst_tick, 1, jnp.where(t < last_tick, BURST_RATE, 2 * per_layer)))
         begin = jnp.where(t < burst_tick, t - first_tick,
-                          jnp.where(t < last_tick, late + 3 * (t - burst_tick), late + 3 * burst))
+                          jnp.where(t < last_tick, late + BURST_RATE * (t - burst_tick), late + BURST_RATE * burst))
 
         def ahead(j, _):
             forward_unit(begin + j, True)
@@ -372,7 +374,7 @@
         lax.fori_loop(0, count, ahead, 0)
 
         for s in (4, 3, 2, 1, 0):
-            stage(t - s, s)
+            stage(t - 1 - s, s)
         return 0
     lax.fori_loop(0, last_tick + 1, tick, 0)
 

time: 1400 us -> 1370 us (0.979)
  Pallas kernels: 1060 us -> 1030 us
    pallas_call x1, Pallas kernels: 1060 us -> 1030 us  [train_step(): kernel(w_first, w_second, m_first, m_second, x_now, y_now, x_next)]
where the time goes in v2:
time: 1370 us
  Pallas kernels  1030 us (75%)
  other arithmetic  331 us (24%)
    pallas_call x1, Pallas kernels, train_step(): kernel(w_first, w_second, m_first, m_second, x_now, y_now, x_next)  1030 us
    sub x1, other arithmetic, train_step(): weight_first = w_first - learn_rate * mom_first  167 us
    sub x1, other arithmetic, train_step(): weight_second = w_second - learn_rate * mom_second  164 us

profile of v2, /device:TPU:0, one launch (start us, length us, event | category | flops | bytes accessed | tf_op | source)
XLA Modules:
  0.0 1368.0 jit_solution(13148665150678279297)
XLA Ops:
  0.6 1034.9 %shard_map.127 = (bf16[12,768,3072]{2,1,0:T(8,128)(2,1)}, bf16[12,3072,768]{2,1,0:T(8,128)(2,1)}, bf16[12,512,768]{2,1,0:T(8,128)(2,1)}, f32[512,768]{1,0:T(8,128)}) custom-call(f32[12,768,3072]{2,1,0:T(8,128)} %w1.1, f32[12,3072,768]{2,1,0:T(8,128)} %w2.1, f32[12,768,3072]{2,1,0:T(8,128)} %m1.1, f32[12,3072,768]{2,1,0:T(8,128)} %m2.1, ...), custom_call_target="tpu_custom_call" | custom-call | tf_op jit(solution)/shard_map/pallas_call | solution.py:434
  1035.5 166.6 %multiply_subtract_fusion.1 = (f32[12,768,3072]{2,1,0:T(8,128)}, f32[12,768,3072]{2,1,0:T(8,128)}) fusion(f32[12,768,3072]{2,1,0:T(8,128)} %w1.1, bf16[12,768,3072]{2,1,0:T(8,128)(2,1)} %get-tuple-element.9, f32[12,768,3072]{2,1,0:T(8,128)} %m1.1), kind=kLoop, calls=%fused_computation.2 | loop fusion | flops 141557760 | bytes 509607936 | tf_op jit(solution)/shard_map/sub | solution.py:437
  1202.1 0.0 copy-start
  1202.1 0.0 copy-start.1
  1202.1 163.9 %multiply_subtract_fusion = (f32[12,3072,768]{2,1,0:T(8,128)}, f32[12,3072,768]{2,1,0:T(8,128)}) fusion(f32[12,3072,768]{2,1,0:T(8,128)} %w2.1, bf16[12,3072,768]{2,1,0:T(8,128)(2,1)} %get-tuple-element.10, f32[12,3072,768]{2,1,0:T(8,128)} %m2.1), kind=kLoop, calls=%fused_computation | loop fusion | flops 141557760 | bytes 509607936 | tf_op jit(solution)/shard_map/sub | solution.py:438
  1366.0 0.0 copy-done
  1366.0 0.0 copy-done.1
  1366.0 0.3 multiply_reduce_fusion
  1366.3 0.6 broadcast_multiply_fusion
  1366.9 1.1 copy.15
Async XLA Ops:
  1202.1 163.9 %copy-start = (f32[512,768]{1,0:T(8,128)S(1)}, f32[512,768]{1,0:T(8,128)}, u32[]{:S(2)}) copy-start(f32[512,768]{1,0:T(8,128)} %get-tuple-element.27) | copy-start | bytes 4718596
  1202.1 163.9 %copy-start.1 = (bf16[512,768]{1,0:T(8,128)(2,1)S(1)}, bf16[512,768]{1,0:T(8,128)(2,1)}, u32[]{:S(2)}) copy-start(bf16[512,768]{1,0:T(8,128)(2,1)} %param.15) | copy-start | bytes 2359300
